TPU v7x, 256 devices: a whole 4x4x8 slice. The times are simulated.
256 devices in a mesh: outer: 8 (over x, y_hi), dp: 32 (over y_lo, z, core).
Axes of the slice: x: 4, y: 4 (y_hi: 2, y_lo: 2; y = y_hi * 2 + y_lo), z: 8, core: 2. Of those that a mesh axis runs over, the one named last changes fastest.
Arguments:
- fast_weights: float32 [8, 4096, 2048], P('outer', 'dp'), may hold values from -6 to 6
- slow_weights: float32 [4096, 2048], P('dp', 'outer'), may hold values from -6 to 6
- momentum: float32 [4096, 2048], P('dp', 'outer'), may hold values from -3 to 3
- tokens: bfloat16 [196608, 4096], P(('outer', 'dp')), may hold values from -6 to 6
- norm_gain: float32 [4096], replicated, may hold values from 0.1 to 1.9
Outputs:
- slow_next: float32 [4096, 2048], P('dp', 'outer')
- momentum_next: float32 [4096, 2048], P('dp', 'outer')
- fast_next: float32 [4096, 2048], P('dp')
- key_values: bfloat16 [196608, 2048], P(('outer', 'dp'))
All inputs are finite; a program needn't handle non-finite values.
Results may differ from a plain program's by a relative error of at most 0.0057.
Values may be sent and summed in bfloat16 or wider, within the bound.
A program may use at most 128 MiB of HBM per device.

v0:
```python
import jax
import jax.numpy as jnp
from jax import lax
from jax.sharding import PartitionSpec as P

OUTER_LR = 0.7
MOMENTUM_COEF = 0.9
EPSILON = 1e-05


def cut_along(shard, dim, size):
    before, after = (shard.shape[:dim], shard.shape[dim + 1 :])
    return jnp.moveaxis(shard.reshape(*before, size, -1, *after), dim, 0)


def summed_on_arrival(shard, axis, dim):
    parts = cut_along(shard, dim, lax.axis_size(axis))
    arrived = lax.all_to_all(parts, axis, split_axis=0, concat_axis=0, tiled=True)
    return arrived.sum(axis=0)


def in_order(parts, dim):
    lengths = list(parts.shape[1:])
    lengths[dim] *= parts.shape[0]
    return jnp.moveaxis(parts, 0, dim).reshape(lengths)


def sent_to_all(shard, axis):
    copies = jnp.broadcast_to(shard, (lax.axis_size(axis), *shard.shape))
    return lax.all_to_all(copies, axis, split_axis=0, concat_axis=0, tiled=True)


def collect(shard, axis, dim):
    return in_order(sent_to_all(shard, axis), dim)


def outer_update(slow_part, moment_part, fast_total, pod_count):
    outer_grad = slow_part - fast_total / pod_count
    moment_next = MOMENTUM_COEF * moment_part + outer_grad
    slow_next = slow_part - OUTER_LR * (outer_grad + MOMENTUM_COEF * moment_next)
    return (slow_next, moment_next)


def body(fast_weights, slow_weights, momentum, tokens, norm_gain):
    pod_count = lax.axis_size("outer")
    width = tokens.shape[1]
    fast_total = summed_on_arrival(fast_weights[0], "outer", 1)
    slow_next, momentum_next = outer_update(slow_weights, momentum, fast_total, pod_count)
    fast_next = collect(slow_next, "outer", 1)
    values = tokens.astype(jnp.float32)
    meansq = jnp.mean(values * values, axis=-1, keepdims=True)
    normed = (values * lax.rsqrt(meansq + EPSILON) * norm_gain).astype(jnp.bfloat16)
    whole_weights = lax.all_gather(fast_next.astype(jnp.bfloat16), "dp", axis=0, tiled=True)
    product = jnp.dot(normed, whole_weights, preferred_element_type=jnp.float32)
    key_values = (product * width ** (-0.5)).astype(jnp.bfloat16)
    return (slow_next, momentum_next, fast_next, key_values)


def solution(mesh):
    in_specs = (
        P("outer", "dp", None),
        P("dp", "outer"),
        P("dp", "outer"),
        P(("outer", "dp"), None),
        P(),
    )
    out_specs = (P("dp", "outer"), P("dp", "outer"), P("dp", None), P(("outer", "dp"), None))
    return jax.shard_map(body, mesh=mesh, in_specs=in_specs, out_specs=out_specs, check_vma=False)
```

profile of v0, /device:TPU:17, one launch (start us, length us, event | category | flops | bytes accessed | tf_op | source)
XLA Modules:
  0.0 206.3 jit_solution(3373704709159486115)
XLA Ops:
  7.2 0.0 copy-start.1
  7.2 0.0 all-gather.2.cloned.1.call-start
  7.2 1.5 copy.9
  8.8 0.3 copy.10
  9.1 20.6 %all_to_all.10 = f32[8,128,256]{2,1,0:T(8,128)S(1)} all-to-all(f32[8,128,256]{2,1,0:T(8,128)S(1)} %copy.10), channel_id=1, replica_groups=mesh['outer'=8,'dp'=32] {'outer'}, dimensions={0} | all-to-all | bytes 2097152 | tf_op jit(solution)/shard_map/all_to_all | solution.py:18
  29.7 0.1 reduce_sum.18
  29.7 1.7 multiply_subtract_fusion
  31.4 0.0 copy-start
  31.4 0.1 broadcast_in_dim.2
  31.5 17.5 %all_to_all.11 = f32[8,128,256]{2,1,0:T(8,128)S(1)} all-to-all(f32[8,128,256]{2,1,0:T(8,128)S(1)} %broadcast_in_dim.2), channel_id=1, replica_groups=mesh['outer'=8,'dp'=32] {'outer'}, dimensions={0} | all-to-all | bytes 2097152 | tf_op jit(solution)/shard_map/all_to_all | solution.py:30
  49.0 0.3 copy.11
  49.3 0.9 bitcast_convert_fusion
  50.1 0.0 all-gather.2.cloned.1.call-update
  50.2 4.1 %fusion = f32[768]{0:T(1024)S(1)} fusion(bf16[768,4096]{1,0:T(8,128)(2,1)} %param.8), kind=kLoop, calls=%fused_computation.2 | loop fusion | flops 9436416 | bytes 6294528 | tf_op jit(solution)/shard_map/reduce_sum | solution.py:51
  54.3 1.3 copy.12
  55.6 124.2 %all-gather.2.cloned.1.call-done = bf16[4096,2048]{0,1:T(8,128)(2,1)} async-done(((bf16[128,2048]{0,1:T(8,128)(2,1)}), bf16[4096,2048]{0,1:T(8,128)(2,1)}) %all-gather.2.cloned.1.call-update) | async-done | bytes 16777232 | tf_op jit(solution)/shard_map/all_gather | solution.py:53
  179.7 0.0 copy-done.1
  179.7 19.7 %multiply_convert_fusion = bf16[768,2048]{1,0:T(8,128)(2,1)} fusion(bf16[4096,2048]{0,1:T(8,128)(2,1)} %all-gather.2.cloned.1.call-done, bf16[768,4096]{1,0:T(8,128)(2,1)} %param.8, f32[4096]{0:T(1024)S(1)} %copy-done.1, f32[768]{0:T(1024)S(1)} %add_rsqrt_fusion), kind=kOutput, calls=%fused_computation.6 | convolution fusion | flops 12900630528 | bytes 26233856 | tf_op jit(solution)/shard_map/dot_general | solution.py:54
  199.5 0.0 copy-done
  (1 shorter events, 0.0 us)
Async XLA Ops:
  7.2 172.6 %copy-start.1 = (f32[4096]{0:T(1024)S(1)}, f32[4096]{0:T(1024)}, u32[]{:S(2)}) copy-start(f32[4096]{0:T(1024)} %param.9) | copy-start | bytes 49156
  7.2 172.6 %all-gather.2.cloned.1.call-start = ((), (), s32[]{:S(2)}) async-start(), calls=%async_computation.2 | async-start | bytes 17301504 | tf_op jit(solution)/shard_map/all_gather | solution.py:53
  31.4 168.1 %copy-start = (f32[128,256]{1,0:T(8,128)}, f32[128,256]{1,0:T(8,128)S(1)}, u32[]{:S(2)}) copy-start(f32[128,256]{1,0:T(8,128)S(1)} %get-tuple-element.8) | copy-start | bytes 393220
Sparse Core Ops, SparseCore 0:
  50.3 129.4 all-gather.1
where the time goes:
time: 207 us; the launch traced here: 206 us
  waiting for transfers between devices  124 us (60%)
  blocking collectives  38 us (18%)
  matrix products  19.7 us (10%)
  between operations  14.1 us (7%)
  other arithmetic  6.66 us (3%)
  local copies, waits for them, and re-layouts  3.61 us (2%)
    all_gather x1, waiting for transfers between devices, body(): lax.all_gather(fast_next.astype(jnp.bfloat16), 'dp', axis=0, tiled=True)  124 us
    all_to_all x1, blocking collectives, summed_on_arrival(): lax.all_to_all(parts, axis, split_axis=0, concat_axis=0, tiled=True)  20.6 us
    dot_general x1, matrix products, body(): product = jnp.dot(normed, whole_weights, preferred_element_type=jnp.float32)  19.7 us
    all_to_all x1, blocking collectives, sent_to_all(): return lax.all_to_all(copies, axis, split_axis=0, concat_axis=0, tiled=True)  17.5 us
  transfers between devices with their start and end apart: 1, of which 1 were waited for; matrix products, arithmetic and copies ran while one was open for 3% of the time, Pallas kernels for 0%

commit v1 on v0

--- a/solution.py
+++ b/solution.py
@@ -50,7 +50,12 @@
     values = tokens.astype(jnp.float32)
     meansq = jnp.mean(values * values, axis=-1, keepdims=True)
     normed = (values * lax.rsqrt(meansq + EPSILON) * norm_gain).astype(jnp.bfloat16)
-    whole_weights = lax.all_gather(fast_next.astype(jnp.bfloat16), "dp", axis=0, tiled=True)
+    whole_weights = jnp.concatenate(
+        lax.all_to_all(
+            jnp.stack([fast_next.astype(jnp.bfloat16)] * lax.axis_size("dp")), "dp", 0, 0
+        ),
+        axis=0,
+    )
     product = jnp.dot(normed, whole_weights, preferred_element_type=jnp.float32)
     key_values = (product * width ** (-0.5)).astype(jnp.bfloat16)
     return (slow_next, momentum_next, fast_next, key_values)

time: 207 us -> 454 us (2.19)
  the two profiles are of different devices: /device:TPU:17 before, /device:TPU:96 now
where the time goes in v1:
time: 454 us
  waiting for transfers between devices  367 us (81%)
  blocking collectives  42.3 us (9%)
  matrix products  19.7 us (4%)
  local copies, waits for them, and re-layouts  9.81 us (2%)
  starting transfers between devices  8.12 us (2%)
  other arithmetic  5.87 us (1%)
    all_to_all x1, waiting for transfers between devices, body(): lax.all_to_all(jnp.stack([fast_next.astype(jnp.bfloat16)] * lax.axis_size...  367 us
    all_to_all x1, blocking collectives, summed_on_arrival(): lax.all_to_all(parts, axis, split_axis=0, concat_axis=0, tiled=True)  23.6 us
    dot_general x1, matrix products, body(): product = jnp.dot(normed, whole_weights, preferred_element_type=jnp.float32)  19.7 us
    all_to_all x1, blocking collectives, sent_to_all(): return lax.all_to_all(copies, axis, split_axis=0, concat_axis=0, tiled=True)  18.7 us
  transfers between devices with their start and end apart: 1, of which 1 were waited for; matrix products, arithmetic and copies ran while one was open for 1% of the time, Pallas kernels for 0%

profile of v1, /device:TPU:96, one launch (start us, length us, event | category | flops | bytes accessed | tf_op | source)
XLA Modules:
  0.0 454.0 jit_solution(14462484436557550798)
XLA Ops:
  0.6 1.5 copy.9
  2.2 0.3 copy.10
  2.5 23.6 %all_to_all.15 = f32[8,128,256]{2,1,0:T(8,128)S(1)} all-to-all(f32[8,128,256]{2,1,0:T(8,128)S(1)} %copy.10), channel_id=1, replica_groups=mesh['outer'=8,'dp'=32] {'outer'}, dimensions={0} | all-to-all | bytes 2097152 | tf_op jit(solution)/shard_map/all_to_all | solution.py:18
  26.1 0.1 reduce_sum.18
  26.2 1.7 multiply_subtract_fusion
  27.8 0.0 copy-start
  27.8 0.1 broadcast_in_dim.2
  27.9 18.7 %all_to_all.16 = f32[8,128,256]{2,1,0:T(8,128)S(1)} all-to-all(f32[8,128,256]{2,1,0:T(8,128)S(1)} %broadcast_in_dim.2), channel_id=1, replica_groups=mesh['outer'=8,'dp'=32] {'outer'}, dimensions={0} | all-to-all | bytes 2097152 | tf_op jit(solution)/shard_map/all_to_all | solution.py:30
  46.6 0.3 copy.11
  47.0 0.1 bitcast_convert_fusion
  47.0 0.2 copy.12
  47.2 6.0 %stack.2 = bf16[32,128,2048]{2,1,0:T(8,128)(2,1)} broadcast(bf16[128,2048]{1,0:T(8,128)(2,1)S(1)} %copy.12), dimensions={1,2} | broadcast | bytes 17301504 | tf_op jit(solution)/shard_map/stack | solution.py:55
  53.2 0.0 copy-done
  53.2 0.0 copy-start.1
  53.2 8.1 %all-to-all-start.2 = ((bf16[32,128,2048]{2,1,0:T(8,128)(2,1)}), bf16[32,128,2048]{2,1,0:T(8,128)(2,1)}, u32[]{:S(2)}, u32[]{:S(2)}) async-start(bf16[32,128,2048]{2,1,0:T(8,128)(2,1)} %stack.2), calls=%async_computation.2 | async-start | bytes 33554432 | tf_op jit(solution)/shard_map/all_to_all | solution.py:54
  61.4 4.1 fusion
  65.4 1.3 copy.13
  66.8 367.5 %all-to-all-done.2 = bf16[32,128,2048]{2,1,0:T(8,128)(2,1)} async-done(((bf16[32,128,2048]{2,1,0:T(8,128)(2,1)}), bf16[32,128,2048]{2,1,0:T(8,128)(2,1)}, u32[]{:S(2)}, u32[]{:S(2)}) %all-to-all-start.2) | async-done | bytes 16777248 | tf_op jit(solution)/shard_map/all_to_all | solution.py:54
  434.2 0.0 copy-done.1
  434.2 19.7 %multiply_convert_fusion = bf16[768,2048]{1,0:T(8,128)(2,1)} fusion(bf16[4096,2048]{1,0:T(8,128)(2,1)} %bitcast.5, bf16[768,4096]{1,0:T(8,128)(2,1)} %param.8, f32[4096]{0:T(1024)S(1)} %copy-done.1, f32[768]{0:T(1024)S(1)} %add_rsqrt_fusion), kind=kOutput, calls=%fused_computation.6 | convolution fusion | flops 12900630528 | bytes 26233856 | tf_op jit(solution)/shard_map/dot_general | solution.py:59
  (1 shorter events, 0.0 us)
Async XLA Ops:
  27.8 25.4 %copy-start = (f32[128,256]{1,0:T(8,128)}, f32[128,256]{1,0:T(8,128)S(1)}, u32[]{:S(2)}) copy-start(f32[128,256]{1,0:T(8,128)S(1)} %get-tuple-element.8) | copy-start | bytes 393220
  53.2 381.0 %copy-start.1 = (f32[4096]{0:T(1024)S(1)}, f32[4096]{0:T(1024)}, u32[]{:S(2)}) copy-start(f32[4096]{0:T(1024)} %param.9) | copy-start | bytes 49156
  53.2 381.0 %all-to-all-start.2 = ((bf16[32,128,2048]{2,1,0:T(8,128)(2,1)}), bf16[32,128,2048]{2,1,0:T(8,128)(2,1)}, u32[]{:S(2)}, u32[]{:S(2)}) async-start(bf16[32,128,2048]{2,1,0:T(8,128)(2,1)} %stack.2), calls=%async_computation.2 | async-start | bytes 33554432 | tf_op jit(solution)/shard_map/all_to_all | solution.py:54
